TPU v7x, 32 devices: a whole 2x2x4 slice. The times are simulated.
32 devices in a mesh: row: 4 (over z), col: 8 (over y, x, core).
Axes of the slice: x: 2, y: 2, z: 4, core: 2. Of those that a mesh axis runs over, the one named last changes fastest.
Arguments:
- response_coeffs: float32 [3, 8192, 1024], P(None, ('row', 'col')), may hold values from -6 to 6
- occupied_coeffs: float32 [8192, 1024], P(('row', 'col')), may hold values from -0.1875 to 0.1875
Outputs:
- density: float32 [3, 8192, 8192], P(None, 'row', 'col')
All inputs are finite; a program needn't handle non-finite values.
Results may differ from a plain program's by a relative error of at most 0.0003.
Values sent between devices are 32-bit elements; how exact they have to be, the bound alone decides.
A program may use at most 256 MiB of HBM per device.

v0:
```python
import functools

import jax
import jax.numpy as jnp
from jax import lax
from jax.experimental import pallas as pl
from jax.experimental.pallas import tpu as pltpu
from jax.sharding import PartitionSpec as P

SLICE_PAIRS = ((0, 0), (0, 1), (1, 0))


def partner(value, axis, stride):
    mask = 2**stride
    pairs = [(source, source ^ mask) for source in range(lax.axis_size(axis))]
    return lax.ppermute(value, axis, pairs)


def split_slices(values):
    leading = lax.optimization_barrier(values.astype(jnp.bfloat16))
    remainder = values - leading.astype(jnp.float32)
    trailing = lax.optimization_barrier(remainder.astype(jnp.bfloat16))
    return [leading, trailing]


def contribute(row_slices, column_slices, perturbations):
    accumulated = jnp.zeros(
        (perturbations, row_slices[0].shape[1], column_slices[0].shape[1]), jnp.float32
    )
    for left_index, right_index in SLICE_PAIRS:
        forward_term = jnp.einsum(
            "kro,co->krc",
            row_slices[left_index][:perturbations],
            column_slices[right_index][perturbations],
            preferred_element_type=jnp.float32,
        )
        mirror_term = jnp.einsum(
            "ro,kco->krc",
            row_slices[right_index][perturbations],
            column_slices[left_index][:perturbations],
            preferred_element_type=jnp.float32,
        )
        accumulated = accumulated + forward_term + mirror_term
    return accumulated


def relay_columns(stacked, perturbations):
    rows_total = lax.axis_size("row")
    columns_total = lax.axis_size("col")
    col_index = lax.axis_index("col")
    shard_rows = stacked.shape[1]
    orbitals = stacked.shape[2]
    half_rows = shard_rows // 2
    swap_bit = rows_total.bit_length() - 1
    own_first = stacked[:, :half_rows]
    partner_second = partner(stacked[:, half_rows:], "col", swap_bit)
    even_first = col_index // rows_total == 0
    leading = jnp.where(even_first, own_first, partner_second)
    trailing = jnp.where(even_first, partner_second, own_first)
    paired = jnp.concatenate([leading, trailing], axis=1)
    gathered = lax.all_gather(paired, "row", axis=1, tiled=True)
    regrouped = lax.all_to_all(gathered, "col", split_axis=1, concat_axis=1, tiled=True)
    shaped = regrouped.reshape(perturbations + 1, 2, rows_total, half_rows, orbitals)
    flipped = shaped[:, ::-1]
    ordered = jnp.where(col_index % 2 == 0, shaped, flipped)
    return jnp.swapaxes(ordered, 1, 2).reshape(
        perturbations + 1, columns_total * half_rows, orbitals
    )


def shards(response_coeffs, occupied_coeffs):
    perturbations = response_coeffs.shape[0]
    stacked = jnp.concatenate([response_coeffs, occupied_coeffs[None]], axis=0)
    column_panel = relay_columns(stacked, perturbations)
    column_slices = split_slices(column_panel)
    return contribute(
        split_slices(lax.all_gather(stacked, "col", axis=1, tiled=True)),
        column_slices,
        perturbations,
    )


HALVES = 2


def flip(value):
    return value + 1 - 2 * (value % 2)


def across(value):
    return value + 2 - 4 * (value // 2)


def panel_kernel(
    resp, occ, out, rowbuf, colbuf,
    row_lead, row_trail, col_lead, col_trail, stage, tile,
    rx_row, rx_col, tx, stage_sem, tile_sem,
):
    perturbations, shard_rows, orbitals = resp.shape
    kinds = perturbations + 1
    piece = shard_rows // HALVES
    pieces = kinds * HALVES
    early = pieces // 2
    positions = 4 * pieces
    block_rows = tile.shape[2]
    row_blocks = 8 * shard_rows // block_rows
    panel_rows = 8 * shard_rows

    z = lax.axis_index("row")
    planes = lax.axis_size("row")
    column = lax.axis_index("col")
    w, core = column // 2, column % 2
    xq, yq, dq = flip(w), across(w), flip(across(w))
    other = 1 - core
    x_dev, y_dev, p_dev = (z, 2 * xq + core), (z, 2 * yq + core), (z, 2 * w + other)
    up_dev, down_dev = (z + 1, column), (z - 1, column)
    has_up, has_down = z < planes - 1, z > 0
    diagonal = z == w
    match = w // 2 == core
    distance = jnp.where(z > w, z - w, w - z)

    barrier = pltpu.get_barrier_semaphore()

    def greet(device):
        pl.semaphore_signal(barrier, inc=1, device_id=device, device_id_type=pl.DeviceIdType.MESH)

    above, below = (z + 1) % planes, (z + planes - 1) % planes
    for device in (x_dev, y_dev, p_dev, (above, column), (below, column)):
        greet(device)
    pl.semaphore_wait(barrier, 5)

    def row_piece(quarter, lane, j):
        return rowbuf.at[2 * quarter + lane, j // HALVES, pl.ds(pl.multiple_of((j % HALVES) * piece, piece), piece)]

    def col_piece(p):
        i, j = p // pieces, p % pieces
        return colbuf.at[i, j // HALVES, pl.ds(pl.multiple_of((j % HALVES) * piece, piece), piece)]

    def send(source, target, send_sem, recv_sem, device):
        pltpu.make_async_remote_copy(
            src_ref=source, dst_ref=target, send_sem=send_sem, recv_sem=recv_sem,
            device_id=device, device_id_type=pl.DeviceIdType.MESH,
        ).start()

    def send_row(quarter, lane, j, slot, device):
        ref = row_piece(quarter, lane, j)
        send(ref, ref, tx.at[slot], rx_row.at[2 * quarter + lane, j], device)

    def wait_row(quarter, lane, j):
        ref = row_piece(quarter, lane, j)
        pltpu.make_async_copy(ref, ref, rx_row.at[2 * quarter + lane, j]).wait()

    load_resp = pltpu.make_async_copy(resp, stage.at[pl.ds(0, perturbations)], stage_sem.at[0])
    load_occ = pltpu.make_async_copy(occ, stage.at[perturbations], stage_sem.at[1])
    load_resp.start()
    load_occ.start()
    for j in range(pieces):
        k, rows = j // HALVES, pl.ds((j % HALVES) * piece, piece)
        source = resp.at[k, rows] if k < perturbations else occ.at[rows]
        for slot, device in ((0, x_dev), (1, y_dev), (4, p_dev)):
            send(source, row_piece(w, core, j), tx.at[slot], rx_row.at[2 * w + core, j], device)
    load_resp.wait()
    load_occ.wait()
    keep = pltpu.make_async_copy(stage, rowbuf.at[2 * w + core], stage_sem.at[0])
    keep.start()
    keep.wait()

    first = jnp.where(match, w, yq)
    second = flip(first)

    def order(i):
        quarter = jnp.where(i < 2, first, second)
        lane = jnp.where(i % 2 == 0, core, other)
        return quarter, lane

    def emit(source, p):
        @pl.when(has_up & (z >= w))
        def _():
            send(source, col_piece(p), tx.at[5], rx_col.at[p], up_dev)

        @pl.when(has_down & (z <= w))
        def _():
            send(source, col_piece(p), tx.at[6], rx_col.at[p], down_dev)

    def emit_own(p):
        quarter, lane = order(p // pieces)
        emit(row_piece(quarter, lane, p % pieces), p)

    def split_into(value, lead, trail, start):
        leading = value.astype(jnp.bfloat16)
        lead[pl.ds(start, shard_rows), :] = leading
        trail[pl.ds(start, shard_rows), :] = (value - leading.astype(jnp.float32)).astype(jnp.bfloat16)

    def load_stage(source):
        copy = pltpu.make_async_copy(source, stage, stage_sem.at[0])
        copy.start()
        copy.wait()

    def tile_copy(slot, block, start):
        return pltpu.make_async_copy(
            tile.at[slot],
            out.at[:, pl.ds(pl.multiple_of(block * block_rows, block_rows), block_rows),
                   pl.ds(pl.multiple_of(start, shard_rows), shard_rows)],
            tile_sem.at[slot],
        )

    gathered = pieces + early
    convert_at = gathered + 1
    matmul_at = convert_at + 8
    rounds = positions + planes - 1
    hidden = 3 * row_blocks
    tasks = 4 * row_blocks

    def step(t, carry):
        @pl.when(t < pieces)
        def _():
            wait_row(xq, core, t)
            send_row(xq, core, t, 4, p_dev)
            wait_row(yq, core, t)
            send_row(yq, core, t, 4, p_dev)
            wait_row(w, other, t)

            @pl.when(t < early)
            def _():
                send_row(yq, core, t, 2, x_dev)

            @pl.when(t >= early)
            def _():
                send_row(xq, core, t, 3, y_dev)

        @pl.when((t >= 1) & (t < pieces + 1))
        def _():
            wait_row(xq, other, t - 1)
            wait_row(yq, other, t - 1)

        @pl.when((t >= pieces) & (t < gathered))
        def _():
            for shift in (0, early):
                wait_row(dq, core, t - pieces + shift)
                send_row(dq, core, t - pieces + shift, 4, p_dev)

        @pl.when((t >= pieces + 1) & (t < gathered + 1))
        def _():
            for shift in (0, early):
                wait_row(dq, other, t - pieces - 1 + shift)

        @pl.when(diagonal & match & (t < positions // 2))
        def _():
            emit_own(2 * t)
            emit_own(2 * t + 1)

        @pl.when(diagonal & (w // 2 != core) & (t < positions))
        def _():
            emit_own(t)

        @pl.when((z != w) & (t >= distance) & (t < positions + distance))
        def _():
            p = t - distance
            ref = col_piece(p)
            pltpu.make_async_copy(ref, ref, rx_col.at[p]).wait()
            emit(ref, p)

        @pl.when((t >= convert_at) & (t < matmul_at))
        def _():
            shard = t - convert_at
            load_stage(rowbuf.at[shard])

            def convert(k, carry):
                start = pl.multiple_of(k * panel_rows + shard * shard_rows, shard_rows)
                split_into(stage[k], row_lead, row_trail, start)
                return carry

            lax.fori_loop(0, kinds, convert, 0)

        @pl.when(((t >= matmul_at) & (t < matmul_at + hidden)) | (t >= rounds))
        def _():
            task = jnp.where(t >= rounds, t - rounds + hidden, t - matmul_at)
            part, block = task // row_blocks, task % row_blocks
            quarter, lane = order(part)

            @pl.when(block == 0)
            def _():
                @pl.when(diagonal)
                def _():
                    load_stage(rowbuf.at[2 * quarter + lane])

                @pl.when(z != w)
                def _():
                    load_stage(colbuf.at[part])

                def convert(k, carry):
                    split_into(stage[k], col_lead, col_trail, pl.multiple_of(k * shard_rows, shard_rows))
                    return carry

                lax.fori_loop(0, kinds, convert, 0)

            slot = task % 2
            place = (2 * (quarter % 2) + lane) * shard_rows

            @pl.when(task >= 2)
            def _():
                tile_copy(slot, block, place).wait()

            def rows_of(ref, k):
                return ref[pl.ds(pl.multiple_of(k * panel_rows + block * block_rows, block_rows), block_rows), :]

            def columns_of(ref, k):
                return ref[pl.ds(pl.multiple_of(k * shard_rows, shard_rows), shard_rows), :]

            def product(left, right):
                return lax.dot_general(left, right, (((1,), (1,)), ((), ())), preferred_element_type=jnp.float32)

            def perturbation(k, carry):
                total = product(rows_of(row_lead, k), columns_of(col_lead, perturbations))
                total += product(rows_of(row_lead, k), columns_of(col_trail, perturbations))
                total += product(rows_of(row_trail, k), columns_of(col_lead, perturbations))
                total += product(rows_of(row_lead, perturbations), columns_of(col_lead, k))
                total += product(rows_of(row_trail, perturbations), columns_of(col_lead, k))
                total += product(rows_of(row_lead, perturbations), columns_of(col_trail, k))
                tile[slot, k] = total
                return carry

            lax.fori_loop(0, perturbations, perturbation, 0)
            tile_copy(slot, block, place).start()

        return carry

    lax.fori_loop(0, rounds + row_blocks, step, 0)

    for slot in range(2):
        tile_copy(slot, 0, 0).wait()

    def drain(slot, ref):
        pltpu.make_async_copy(ref, ref, tx.at[slot]).wait()

    drain(0, rowbuf.at[0])
    drain(1, rowbuf.at[0])
    drain(2, rowbuf.at[0, pl.ds(0, kinds // 2)])
    drain(3, rowbuf.at[0, pl.ds(0, kinds // 2)])
    drain(4, rowbuf.at[pl.ds(0, 4)])

    @pl.when(has_up & (z >= w))
    def _():
        drain(5, rowbuf.at[pl.ds(0, 4)])

    @pl.when(has_down & (z <= w))
    def _():
        drain(6, rowbuf.at[pl.ds(0, 4)])


def panels(response_coeffs, occupied_coeffs):
    perturbations, shard_rows, orbitals = response_coeffs.shape
    kinds = perturbations + 1
    pieces = kinds * HALVES
    block_rows = 2 * shard_rows
    any_space = pl.BlockSpec(memory_space=pl.ANY)
    float32, bfloat16 = jnp.float32, jnp.bfloat16
    return pl.pallas_call(
        panel_kernel,
        out_shape=(
            jax.ShapeDtypeStruct((perturbations, 8 * shard_rows, 4 * shard_rows), float32),
            jax.ShapeDtypeStruct((8, kinds, shard_rows, orbitals), float32),
            jax.ShapeDtypeStruct((4, kinds, shard_rows, orbitals), float32),
        ),
        in_specs=[any_space] * 2,
        out_specs=(any_space,) * 3,
        scratch_shapes=[
            pltpu.VMEM((kinds * 8 * shard_rows, orbitals), bfloat16),
            pltpu.VMEM((kinds * 8 * shard_rows, orbitals), bfloat16),
            pltpu.VMEM((kinds * shard_rows, orbitals), bfloat16),
            pltpu.VMEM((kinds * shard_rows, orbitals), bfloat16),
            pltpu.VMEM((kinds, shard_rows, orbitals), float32),
            pltpu.VMEM((2, perturbations, block_rows, shard_rows), float32),
            pltpu.SemaphoreType.DMA((8, pieces)),
            pltpu.SemaphoreType.DMA((4 * pieces,)),
            pltpu.SemaphoreType.DMA((7,)),
            pltpu.SemaphoreType.DMA((2,)),
            pltpu.SemaphoreType.DMA((2,)),
        ],
        compiler_params=pltpu.CompilerParams(
            collective_id=0, has_side_effects=True, vmem_limit_bytes=66_000_000
        ),
    )(response_coeffs, occupied_coeffs)[0]


def solution(mesh):
    fits = mesh.shape["row"] == 4 and mesh.shape["col"] == 8
    return jax.shard_map(
        panels if fits else shards,
        mesh=mesh,
        in_specs=(P(None, ("row", "col"), None), P(("row", "col"), None)),
        out_specs=P(None, "row", "col"),
        check_vma=False,
    )
```

profile of v0, /device:TPU:24, one launch (start us, length us, event | category | flops | bytes accessed | tf_op | source)
XLA Modules:
  0.0 447.7 jit_solution(8263430155668844971)
XLA Ops:
  0.0 430.0 %shard_map.28 = (f32[3,2048,1024]{2,1,0:T(8,128)}, f32[8,4,256,1024]{3,2,1,0:T(8,128)}, f32[4,4,256,1024]{3,2,1,0:T(8,128)}) custom-call(f32[3,256,1024]{2,1,0:T(8,128)} %resp.1, f32[256,1024]{1,0:T(8,128)} %occ.1), custom_call_target="tpu_custom_call" | custom-call | tf_op jit(solution)/shard_map/pallas_call | solution.py:358
  430.0 17.7 %copy.4 = f32[3,2048,1024]{2,1,0:T(8,128)} copy(f32[3,2048,1024]{2,1,0:T(8,128)} %get-tuple-element.6) | data formatting | bytes 50331648
where the time goes:
time: 448 us
  Pallas kernels  430 us (96%)
  local copies, waits for them, and re-layouts  17.7 us (4%)
    pallas_call x1, Pallas kernels, panels(): pl.pallas_call(panel_kernel, out_shape=(jax.ShapeDtypeStruct((perturbatio...  430 us
    unnamed x1, local copies, waits for them, and re-layouts  17.7 us

commit v1 on v0

v1 whole, which is shorter than its diff:
```python
import functools

import jax
import jax.numpy as jnp
from jax import lax
from jax.experimental import pallas as pl
from jax.experimental.pallas import tpu as pltpu
from jax.sharding import PartitionSpec as P

SLICE_PAIRS = ((0, 0), (0, 1), (1, 0))


def partner(value, axis, stride):
    mask = 2**stride
    pairs = [(source, source ^ mask) for source in range(lax.axis_size(axis))]
    return lax.ppermute(value, axis, pairs)


def split_slices(values):
    leading = lax.optimization_barrier(values.astype(jnp.bfloat16))
    remainder = values - leading.astype(jnp.float32)
    trailing = lax.optimization_barrier(remainder.astype(jnp.bfloat16))
    return [leading, trailing]


def contribute(row_slices, column_slices, perturbations):
    accumulated = jnp.zeros(
        (perturbations, row_slices[0].shape[1], column_slices[0].shape[1]), jnp.float32
    )
    for left_index, right_index in SLICE_PAIRS:
        forward_term = jnp.einsum(
            "kro,co->krc",
            row_slices[left_index][:perturbations],
            column_slices[right_index][perturbations],
            preferred_element_type=jnp.float32,
        )
        mirror_term = jnp.einsum(
            "ro,kco->krc",
            row_slices[right_index][perturbations],
            column_slices[left_index][:perturbations],
            preferred_element_type=jnp.float32,
        )
        accumulated = accumulated + forward_term + mirror_term
    return accumulated


def relay_columns(stacked, perturbations):
    rows_total = lax.axis_size("row")
    columns_total = lax.axis_size("col")
    col_index = lax.axis_index("col")
    shard_rows = stacked.shape[1]
    orbitals = stacked.shape[2]
    half_rows = shard_rows // 2
    swap_bit = rows_total.bit_length() - 1
    own_first = stacked[:, :half_rows]
    partner_second = partner(stacked[:, half_rows:], "col", swap_bit)
    even_first = col_index // rows_total == 0
    leading = jnp.where(even_first, own_first, partner_second)
    trailing = jnp.where(even_first, partner_second, own_first)
    paired = jnp.concatenate([leading, trailing], axis=1)
    gathered = lax.all_gather(paired, "row", axis=1, tiled=True)
    regrouped = lax.all_to_all(gathered, "col", split_axis=1, concat_axis=1, tiled=True)
    shaped = regrouped.reshape(perturbations + 1, 2, rows_total, half_rows, orbitals)
    flipped = shaped[:, ::-1]
    ordered = jnp.where(col_index % 2 == 0, shaped, flipped)
    return jnp.swapaxes(ordered, 1, 2).reshape(
        perturbations + 1, columns_total * half_rows, orbitals
    )


def shards(response_coeffs, occupied_coeffs):
    perturbations = response_coeffs.shape[0]
    stacked = jnp.concatenate([response_coeffs, occupied_coeffs[None]], axis=0)
    column_panel = relay_columns(stacked, perturbations)
    column_slices = split_slices(column_panel)
    return contribute(
        split_slices(lax.all_gather(stacked, "col", axis=1, tiled=True)),
        column_slices,
        perturbations,
    )


CUTS = 4


def flip(value):
    return value + 1 - 2 * (value % 2)


def across(value):
    return value + 2 - 4 * (value // 2)


def panel_kernel(
    resp, occ, out, rowbuf, colbuf, straybuf,
    row_lead, row_trail, col_lead, col_trail, stage, acc,
    rx_row, rx_col, rx_stray, tx, stage_sem, acc_sem,
):
    perturbations, shard_rows, orbitals = resp.shape
    kinds = perturbations + 1
    cut = shard_rows // CUTS
    pieces = kinds * CUTS
    early = pieces // 2
    panel_rows = 8 * shard_rows
    block_rows = 2 * shard_rows
    row_blocks = panel_rows // block_rows

    z = lax.axis_index("row")
    planes = lax.axis_size("row")
    column = lax.axis_index("col")
    w, core = column // 2, column % 2
    xq, yq, dq = flip(w), across(w), flip(across(w))
    other = 1 - core
    x_dev, y_dev, p_dev = (z, 2 * xq + core), (z, 2 * yq + core), (z, 2 * w + other)
    up_dev, down_dev = (z + 1, column), (z - 1, column)
    has_up, has_down = z < planes - 1, z > 0
    diagonal = z == w
    match = w // 2 == core
    distance = jnp.where(z > w, z - w, w - z)

    lone = ((z > w) & (core == 1)) | ((z < w) & (core == 0))
    total_up = jnp.where(core == 0, 4 * pieces, 2 * pieces)
    total_down = jnp.where(core == 1, 4 * pieces, 2 * pieces)
    total_in = jnp.where(lone, 2 * pieces, 4 * pieces)

    rising = w == 3
    outer = rising | (w == 0)
    depth = jnp.where(rising, z, planes - 1 - z)
    side = jnp.where(rising, core, other)
    lone_core = jnp.where(rising, 1, 0)
    onward_dev = (jnp.where(rising, z + 1, z - 1), column)
    inbound = outer & (depth > 0)
    onward = outer & (depth < planes - 1)
    relay = ((w == 1) & (core == 1)) | ((w == 2) & (core == 0))

    barrier = pltpu.get_barrier_semaphore()

    def greet(device):
        pl.semaphore_signal(barrier, inc=1, device_id=device, device_id_type=pl.DeviceIdType.MESH)

    for device in (x_dev, y_dev, p_dev, (z, 2 * xq + other), (z, 2 * yq + other)):
        greet(device)

    @pl.when(has_up)
    def _():
        greet(up_dev)

    @pl.when(has_down)
    def _():
        greet(down_dev)

    pl.semaphore_wait(barrier, 5 + jnp.where(has_up, 1, 0) + jnp.where(has_down, 1, 0))

    def rows_at(j):
        return pl.ds(pl.multiple_of((j % CUTS) * cut, cut), cut)

    def row_piece(quarter, lane, j):
        return rowbuf.at[2 * quarter + lane, j // CUTS, rows_at(j)]

    def col_piece(p):
        i, j = p // pieces, p % pieces
        return colbuf.at[i, j // CUTS, rows_at(j)]

    def stray_piece(q, j):
        return straybuf.at[q, j // CUTS, rows_at(j)]

    def send(source, target, send_sem, recv_sem, device):
        pltpu.make_async_remote_copy(
            src_ref=source, dst_ref=target, send_sem=send_sem, recv_sem=recv_sem,
            device_id=device, device_id_type=pl.DeviceIdType.MESH,
        ).start()

    def send_row(quarter, lane, j, slot, device):
        ref = row_piece(quarter, lane, j)
        send(ref, ref, tx.at[slot], rx_row.at[2 * quarter + lane, j], device)

    def arrived(ref, sem):
        pltpu.make_async_copy(ref, ref, sem).wait()

    def wait_row(quarter, lane, j):
        arrived(row_piece(quarter, lane, j), rx_row.at[2 * quarter + lane, j])

    def wait_col(p):
        arrived(col_piece(p), rx_col.at[p])

    load_resp = pltpu.make_async_copy(resp, stage.at[pl.ds(1, perturbations)], stage_sem.at[0])
    load_occ = pltpu.make_async_copy(occ, stage.at[0], stage_sem.at[1])
    load_resp.start()
    load_occ.start()

    def launch(source, j):
        for slot, device in ((0, x_dev), (1, y_dev), (4, p_dev)):
            send(source, row_piece(w, core, j), tx.at[slot], rx_row.at[2 * w + core, j], device)

        @pl.when(diagonal & match & has_up)
        def _():
            send(source, col_piece(j), tx.at[5], rx_col.at[j], up_dev)

        @pl.when(diagonal & match & has_down)
        def _():
            send(source, col_piece(j), tx.at[6], rx_col.at[j], down_dev)

        @pl.when(outer & ((depth == 0) | ((depth == 2) & (side == 1))))
        def _():
            send(source, stray_piece(depth, j), tx.at[7], rx_stray.at[depth, j], onward_dev)

    def launch_occ(j, carry):
        launch(occ.at[rows_at(j)], j)
        return carry

    def launch_resp(j, carry):
        launch(resp.at[j // CUTS - 1, rows_at(j)], j)
        return carry

    lax.fori_loop(0, CUTS, launch_occ, 0)
    lax.fori_loop(CUTS, pieces, launch_resp, 0)
    load_resp.wait()
    load_occ.wait()
    keep = pltpu.make_async_copy(stage, rowbuf.at[2 * w + core], stage_sem.at[0])
    keep.start()
    keep.wait()

    first = jnp.where(match, w, yq)
    second = flip(first)
    early_lane = jnp.where(lone, 1 - w % 2, core)

    def order(i):
        quarter = jnp.where(i < 2, first, second)
        lead = jnp.where(i < 2, core, early_lane)
        lane = jnp.where(i % 2 == 0, lead, 1 - lead)
        return quarter, lane

    def emit(source, p):
        @pl.when(has_up & (z >= w) & (p < total_up))
        def _():
            send(source, col_piece(p), tx.at[5], rx_col.at[p], up_dev)

        @pl.when(has_down & (z <= w) & (p < total_down))
        def _():
            send(source, col_piece(p), tx.at[6], rx_col.at[p], down_dev)

    def emit_own(p, carry):
        quarter, lane = order(p // pieces)
        emit(row_piece(quarter, lane, p % pieces), p)
        return carry

    def pass_on(p, carry):
        wait_col(p)
        emit(col_piece(p), p)
        return carry

    def clip(value, most):
        return jnp.minimum(jnp.maximum(value, 0), most)

    def surplus(value):
        return jnp.maximum(value, 0)

    def sent(t):
        fast = pieces + 1 + t + surplus(t - pieces + 1)
        slow = t + 1 + surplus(t - 2 * pieces + 1)
        return clip(jnp.where(match, fast, slow), 4 * pieces)

    def received(t):
        lagged = t - distance + 1
        return clip(lagged + 1 + surplus(lagged - 2 * pieces + 1), total_in)

    def stray_order(i):
        b = i // pieces
        return jnp.where((depth == 3) & (side == 1), (b + 2) % 3, b)

    last = 3 * pieces
    late = (depth == 3) & (side == 0)
    stray_shift = jnp.where(depth == 1, 1, jnp.where(late, -1, 0))

    def stray_received(t):
        extra = jnp.where(late, surplus(t - last + 1), 0)
        return clip(t + stray_shift + extra, depth * pieces)

    def stray_spread(t):
        return clip(2 * (t - pieces + 1), stray_received(t))

    def take_stray(i, carry):
        q, j = stray_order(i), i % pieces
        ref = stray_piece(q, j)
        arrived(ref, rx_stray.at[q, j])

        @pl.when(onward)
        def _():
            send(ref, ref, tx.at[7], rx_stray.at[q, j], onward_dev)

        return carry

    def late_slot(chip, lane):
        return 2 + jnp.where(lane == 1 - chip % 2, 0, 1)

    def spread_stray(i, carry):
        q, j = stray_order(i), i % pieces
        source = stray_piece(q, j)
        through = jnp.where(rising, 0, 1)

        @pl.when(q == 0)
        def _():
            chip = jnp.where(side == 0, xq, yq)
            send(source, stray_piece(through, j), tx.at[8], rx_stray.at[through, j], (z, 2 * chip + core))

        @pl.when(q > 0)
        def _():
            chip = jnp.where(q == 1, yq, xq)
            p = late_slot(chip, core) * pieces + j
            send(source, col_piece(p), tx.at[8], rx_col.at[p], (z, 2 * chip + lone_core))

        return carry

    def split_into(value, lead, trail, start):
        leading = value.astype(jnp.bfloat16)
        lead[pl.ds(start, shard_rows), :] = leading
        trail[pl.ds(start, shard_rows), :] = (value - leading.astype(jnp.float32)).astype(jnp.bfloat16)

    def acc_copy(k, start):
        return pltpu.make_async_copy(
            acc.at[k],
            out.at[k, :, pl.ds(pl.multiple_of(start, shard_rows), shard_rows)],
            acc_sem.at[k],
        )

    quanta = row_blocks + perturbations
    base = pieces + early + 3
    times = []
    for gap in (0, 1, 1, 2, 3, 3, 4, 5, 6, 6, 7, 8, 8, 9):
        times.append(base + gap)
    for gap in (11, 11, 10, 10, 9, 8, 7):
        times.append(last - gap)
    for gap in (6, 6, 5, 5, 4, 3, 1):
        times.append(last - gap)
    compute_lag = jnp.where(diagonal, 0, jnp.where(lone, 1, distance - 1))

    def done(t):
        count = 0
        for time in times:
            count = count + jnp.where(t - compute_lag >= time, 1, 0)
        return count

    def block_of(ref, kind, block):
        return ref[pl.ds(pl.multiple_of(kind * panel_rows + block * block_rows, block_rows), block_rows), :]

    def product(left, right):
        return lax.dot_general(left, right, (((1,), (1,)), ((), ())), preferred_element_type=jnp.float32)

    def total(kind, block):
        lead, trail = block_of(row_lead, kind, block), block_of(row_trail, kind, block)
        value = product(lead, col_lead[...])
        value += product(lead, col_trail[...])
        value += product(trail, col_lead[...])
        return value

    def target(block):
        return pl.ds(pl.multiple_of(block * block_rows, block_rows), block_rows)

    def quantum(g, carry):
        slot, q = g // quanta, g % quanta
        opening = q < row_blocks
        kind = jnp.where(opening, 0, q - row_blocks + 1)
        quarter, lane = order(slot)
        place = (2 * (quarter % 2) + lane) * shard_rows

        @pl.when((q == 0) | (q >= row_blocks))
        def _():
            @pl.when(lone & (slot >= 2))
            def _():
                def late_wait(j, carry):
                    wait_col(slot * pieces + kind * CUTS + j)
                    return carry

                lax.fori_loop(0, CUTS, late_wait, 0)

            def fetch(source):
                copy = pltpu.make_async_copy(source, stage.at[0], stage_sem.at[0])
                copy.start()
                copy.wait()

            @pl.when(diagonal)
            def _():
                fetch(rowbuf.at[2 * quarter + lane, kind])

            @pl.when(z != w)
            def _():
                fetch(colbuf.at[slot, kind])

            split_into(stage[0], col_lead, col_trail, 0)

        @pl.when((q == 0) & (slot >= 1))
        def _():
            for k in range(perturbations):
                acc_copy(k, place).wait()

        @pl.when(opening)
        def _():
            def start(k, carry):
                acc[k, target(q), :] = total(k + 1, q)
                return carry

            lax.fori_loop(0, perturbations, start, 0)

        @pl.when(q >= row_blocks)
        def _():
            k = q - row_blocks

            def finish(block, carry):
                acc[k, target(block), :] += total(0, block)
                return carry

            lax.fori_loop(0, row_blocks, finish, 0)
            acc_copy(k, place).start()

        return carry

    def step(t, carry):
        @pl.when(t < pieces)
        def _():
            wait_row(xq, core, t)
            send_row(xq, core, t, 4, p_dev)
            wait_row(yq, core, t)
            send_row(yq, core, t, 4, p_dev)
            wait_row(w, other, t)

            @pl.when(t < early)
            def _():
                send_row(yq, core, t, 2, x_dev)

            @pl.when(t >= early)
            def _():
                send_row(xq, core, t, 3, y_dev)

        @pl.when((t >= 1) & (t < pieces + 1))
        def _():
            wait_row(xq, other, t - 1)
            wait_row(yq, other, t - 1)

        @pl.when((t >= pieces) & (t < pieces + early))
        def _():
            for shift in (0, early):
                wait_row(dq, core, t - pieces + shift)
                send_row(dq, core, t - pieces + shift, 4, p_dev)

        @pl.when((t >= pieces + 1) & (t < pieces + early + 1))
        def _():
            for shift in (0, early):
                wait_row(dq, other, t - pieces - 1 + shift)

        @pl.when(diagonal)
        def _():
            opened = jnp.where(match, pieces, 0)
            lax.fori_loop(jnp.where(t == 0, opened, sent(t - 1)), sent(t), emit_own, 0)

        @pl.when(z != w)
        def _():
            lax.fori_loop(received(t - 1), received(t), pass_on, 0)

        @pl.when(inbound)
        def _():
            lax.fori_loop(stray_received(t - 1), stray_received(t), take_stray, 0)
            lax.fori_loop(stray_spread(t - 1), stray_spread(t), spread_stray, 0)

        @pl.when(outer & (depth == 1) & (t >= pieces) & (t < 2 * pieces))
        def _():
            j = t - pieces
            send(row_piece(xq, core, j), stray_piece(1, j), tx.at[7], rx_stray.at[1, j], onward_dev)

        @pl.when(outer & (depth == 2) & (side == 0) & (t >= 2 * pieces) & (t < 2 * pieces + early))
        def _():
            for shift in range(2):
                j = 2 * (t - 2 * pieces) + shift
                send(row_piece(w, core, j), stray_piece(2, j), tx.at[7], rx_stray.at[2, j], onward_dev)

        hop = t - pieces - early - 2

        @pl.when(relay & (hop >= 0) & (hop < pieces))
        def _():
            for through, chip, lone_at, here, slot in ((0, 0, 1, has_down, 9), (1, 3, 0, has_up, 10)):
                @pl.when(here)
                def _():
                    ref = stray_piece(through, hop)
                    arrived(ref, rx_stray.at[through, hop])
                    p = late_slot(chip, core) * pieces + hop
                    send(ref, col_piece(p), tx.at[slot], rx_col.at[p], (z, 2 * chip + lone_at))

        m = jnp.where(t < pieces + early + 1, t - pieces - 1, t - pieces - early + 5)

        @pl.when((m >= 0) & (m < 8) & ((m >= 6) == (t >= pieces + early + 1)))
        def _():
            quarter = jnp.where(m < 2, w, jnp.where(m < 4, xq, jnp.where(m < 6, yq, dq)))
            shard = 2 * quarter + m % 2
            copy = pltpu.make_async_copy(rowbuf.at[shard], stage, stage_sem.at[0])
            copy.start()
            copy.wait()

            def convert(k, carry):
                start = pl.multiple_of(k * panel_rows + shard * shard_rows, shard_rows)
                split_into(stage[k], row_lead, row_trail, start)
                return carry

            lax.fori_loop(0, kinds, convert, 0)

        lax.fori_loop(done(t - 1), done(t), quantum, 0)
        return carry

    lax.fori_loop(0, last + 2, step, 0)

    for k in range(perturbations):
        acc_copy(k, 0).wait()

    def drain(slot, ref):
        pltpu.make_async_copy(ref, ref, tx.at[slot]).wait()

    def drain_shards(slot, count, condition):
        @pl.when(condition)
        def _():
            drain(slot, rowbuf.at[pl.ds(0, count)])

    drain(0, rowbuf.at[0])
    drain(1, rowbuf.at[0])
    drain(2, rowbuf.at[0, pl.ds(0, kinds // 2)])
    drain(3, rowbuf.at[0, pl.ds(0, kinds // 2)])
    drain(4, rowbuf.at[pl.ds(0, 4)])
    drain_shards(5, 4, has_up & (z >= w) & (core == 0))
    drain_shards(5, 2, has_up & (z >= w) & (core == 1))
    drain_shards(6, 4, has_down & (z <= w) & (core == 1))
    drain_shards(6, 2, has_down & (z <= w) & (core == 0))
    for count in (1, 2, 3):
        drain_shards(7, count, outer & (depth == count - 1))
        drain_shards(8, count, outer & (depth == count))
    drain_shards(9, 1, relay & has_down)
    drain_shards(10, 1, relay & has_up)


def panels(response_coeffs, occupied_coeffs):
    perturbations, shard_rows, orbitals = response_coeffs.shape
    kinds = perturbations + 1
    pieces = kinds * CUTS
    any_space = pl.BlockSpec(memory_space=pl.ANY)
    float32, bfloat16 = jnp.float32, jnp.bfloat16
    return pl.pallas_call(
        panel_kernel,
        out_shape=(
            jax.ShapeDtypeStruct((perturbations, 8 * shard_rows, 4 * shard_rows), float32),
            jax.ShapeDtypeStruct((8, kinds, shard_rows, orbitals), float32),
            jax.ShapeDtypeStruct((4, kinds, shard_rows, orbitals), float32),
            jax.ShapeDtypeStruct((3, kinds, shard_rows, orbitals), float32),
        ),
        in_specs=[any_space] * 2,
        out_specs=(any_space,) * 4,
        scratch_shapes=[
            pltpu.VMEM((kinds * 8 * shard_rows, orbitals), bfloat16),
            pltpu.VMEM((kinds * 8 * shard_rows, orbitals), bfloat16),
            pltpu.VMEM((shard_rows, orbitals), bfloat16),
            pltpu.VMEM((shard_rows, orbitals), bfloat16),
            pltpu.VMEM((kinds, shard_rows, orbitals), float32),
            pltpu.VMEM((perturbations, 8 * shard_rows, shard_rows), float32),
            pltpu.SemaphoreType.DMA((8, pieces)),
            pltpu.SemaphoreType.DMA((4 * pieces,)),
            pltpu.SemaphoreType.DMA((3, pieces)),
            pltpu.SemaphoreType.DMA((11,)),
            pltpu.SemaphoreType.DMA((2,)),
            pltpu.SemaphoreType.DMA((perturbations,)),
        ],
        compiler_params=pltpu.CompilerParams(
            collective_id=0, has_side_effects=True, vmem_limit_bytes=66_000_000
        ),
    )(response_coeffs, occupied_coeffs)[0]


def solution(mesh):
    fits = mesh.shape["row"] == 4 and mesh.shape["col"] == 8
    return jax.shard_map(
        panels if fits else shards,
        mesh=mesh,
        in_specs=(P(None, ("row", "col"), None), P(("row", "col"), None)),
        out_specs=P(None, "row", "col"),
        check_vma=False,
    )
```

time: 448 us -> 433 us (0.967)
  the two profiles are of different devices: /device:TPU:24 before, /device:TPU:29 now
where the time goes in v1:
time: 433 us; the launch traced here: 432 us
  Pallas kernels  414 us (96%)
  local copies, waits for them, and re-layouts  17.7 us (4%)
    pallas_call x1, Pallas kernels, panels(): pl.pallas_call(panel_kernel, out_shape=(jax.ShapeDtypeStruct((perturbatio...  414 us
    unnamed x1, local copies, waits for them, and re-layouts  17.7 us

profile of v1, /device:TPU:29, one launch (start us, length us, event | category | flops | bytes accessed | tf_op | source)
XLA Modules:
  0.0 432.2 jit_solution(17507258449164997648)
XLA Ops:
  0.0 414.5 %shard_map.28 = (f32[3,2048,1024]{2,1,0:T(8,128)}, f32[8,4,256,1024]{3,2,1,0:T(8,128)}, f32[4,4,256,1024]{3,2,1,0:T(8,128)}, f32[3,4,256,1024]{3,2,1,0:T(8,128)}) custom-call(f32[3,256,1024]{2,1,0:T(8,128)} %resp.1, f32[256,1024]{1,0:T(8,128)} %occ.1), custom_call_target="tpu_custom_call" | custom-call | tf_op jit(solution)/shard_map/pallas_call | solution.py:542
  414.5 17.7 %copy.4 = f32[3,2048,1024]{2,1,0:T(8,128)} copy(f32[3,2048,1024]{2,1,0:T(8,128)} %get-tuple-element.6) | data formatting | bytes 50331648

commit v2 on v1

--- a/solution.py
+++ b/solution.py
@@ -102,7 +102,7 @@
     pieces = kinds * CUTS
     early = pieces // 2
     panel_rows = 8 * shard_rows
-    block_rows = 2 * shard_rows
+    block_rows = panel_rows // 2
     row_blocks = panel_rows // block_rows
 
     z = lax.axis_index("row")
@@ -119,9 +119,6 @@
     distance = jnp.where(z > w, z - w, w - z)
 
     lone = ((z > w) & (core == 1)) | ((z < w) & (core == 0))
-    total_up = jnp.where(core == 0, 4 * pieces, 2 * pieces)
-    total_down = jnp.where(core == 1, 4 * pieces, 2 * pieces)
-    total_in = jnp.where(lone, 2 * pieces, 4 * pieces)
 
     rising = w == 3
     outer = rising | (w == 0)
@@ -131,7 +128,7 @@
     onward_dev = (jnp.where(rising, z + 1, z - 1), column)
     inbound = outer & (depth > 0)
     onward = outer & (depth < planes - 1)
-    relay = ((w == 1) & (core == 1)) | ((w == 2) & (core == 0))
+    relay = (w == 1) | (w == 2)
 
     barrier = pltpu.get_barrier_semaphore()
 
@@ -157,9 +154,8 @@
     def row_piece(quarter, lane, j):
         return rowbuf.at[2 * quarter + lane, j // CUTS, rows_at(j)]
 
-    def col_piece(p):
-        i, j = p // pieces, p % pieces
-        return colbuf.at[i, j // CUTS, rows_at(j)]
+    def col_piece(slot, j):
+        return colbuf.at[slot, j // CUTS, rows_at(j)]
 
     def stray_piece(q, j):
         return straybuf.at[q, j // CUTS, rows_at(j)]
@@ -180,8 +176,11 @@
     def wait_row(quarter, lane, j):
         arrived(row_piece(quarter, lane, j), rx_row.at[2 * quarter + lane, j])
 
-    def wait_col(p):
-        arrived(col_piece(p), rx_col.at[p])
+    def wait_col(slot, j):
+        arrived(col_piece(slot, j), rx_col.at[slot, j])
+
+    def send_col(source, slot, j, way, device):
+        send(source, col_piece(slot, j), tx.at[way], rx_col.at[slot, j], device)
 
     load_resp = pltpu.make_async_copy(resp, stage.at[pl.ds(1, perturbations)], stage_sem.at[0])
     load_occ = pltpu.make_async_copy(occ, stage.at[0], stage_sem.at[1])
@@ -194,11 +193,11 @@
 
         @pl.when(diagonal & match & has_up)
         def _():
-            send(source, col_piece(j), tx.at[5], rx_col.at[j], up_dev)
+            send_col(source, 0, j, 5, up_dev)
 
         @pl.when(diagonal & match & has_down)
         def _():
-            send(source, col_piece(j), tx.at[6], rx_col.at[j], down_dev)
+            send_col(source, 0, j, 6, down_dev)
 
         @pl.when(outer & ((depth == 0) | ((depth == 2) & (side == 1))))
         def _():
@@ -225,59 +224,75 @@
     early_lane = jnp.where(lone, 1 - w % 2, core)
 
     def order(i):
-        quarter = jnp.where(i < 2, first, second)
-        lead = jnp.where(i < 2, core, early_lane)
-        lane = jnp.where(i % 2 == 0, lead, 1 - lead)
+        double_first = (i == 0) | (i == 3)
+        quarter = jnp.where(lone, jnp.where(i < 2, first, second), jnp.where(double_first, first, second))
+        lone_lane = jnp.where(i < 2, core, early_lane)
+        lone_lane = jnp.where(i % 2 == 0, lone_lane, 1 - lone_lane)
+        lane = jnp.where(lone, lone_lane, jnp.where(i < 2, core, other))
         return quarter, lane
 
-    def emit(source, p):
-        @pl.when(has_up & (z >= w) & (p < total_up))
-        def _():
-            send(source, col_piece(p), tx.at[5], rx_col.at[p], up_dev)
-
-        @pl.when(has_down & (z <= w) & (p < total_down))
-        def _():
-            send(source, col_piece(p), tx.at[6], rx_col.at[p], down_dev)
+    def chain_order(b, double):
+        quarter = jnp.where(b == 0, first, jnp.where(double, second, jnp.where(b == 1, first, across(first))))
+        lane = jnp.where(jnp.where(double, b == 2, b == 1), other, core)
+        return quarter, lane
+
+    def chain_slot(b, double):
+        return jnp.where(double | (b < 2), b, 4)
 
     def emit_own(p, carry):
-        quarter, lane = order(p // pieces)
-        emit(row_piece(quarter, lane, p % pieces), p)
+        b, j = p // pieces, p % pieces
+
+        @pl.when(has_up)
+        def _():
+            quarter, lane = chain_order(b, core == 0)
+            send_col(row_piece(quarter, lane, j), chain_slot(b, core == 0), j, 5, up_dev)
+
+        @pl.when(has_down)
+        def _():
+            quarter, lane = chain_order(b, core == 1)
+            send_col(row_piece(quarter, lane, j), chain_slot(b, core == 1), j, 6, down_dev)
+
         return carry
 
     def pass_on(p, carry):
-        wait_col(p)
-        emit(col_piece(p), p)
+        b, j = p // pieces, p % pieces
+        slot = chain_slot(b, jnp.logical_not(lone))
+        wait_col(slot, j)
+        source = col_piece(slot, j)
+
+        @pl.when(has_up & (z > w))
+        def _():
+            send_col(source, slot, j, 5, up_dev)
+
+        @pl.when(has_down & (z < w))
+        def _():
+            send_col(source, slot, j, 6, down_dev)
+
+        @pl.when(slot == 4)
+        def _():
+            send_col(source, 3, j, 9, p_dev)
+
         return carry
 
     def clip(value, most):
         return jnp.minimum(jnp.maximum(value, 0), most)
 
-    def surplus(value):
-        return jnp.maximum(value, 0)
+    last = 3 * pieces
 
     def sent(t):
-        fast = pieces + 1 + t + surplus(t - pieces + 1)
-        slow = t + 1 + surplus(t - 2 * pieces + 1)
-        return clip(jnp.where(match, fast, slow), 4 * pieces)
+        slow = t + 1 + jnp.maximum(t - pieces - early, 0)
+        return clip(jnp.where(match, pieces + t + 1, slow), last)
 
     def received(t):
-        lagged = t - distance + 1
-        return clip(lagged + 1 + surplus(lagged - 2 * pieces + 1), total_in)
+        return clip(t - distance + 2, last)
 
     def stray_order(i):
         b = i // pieces
         return jnp.where((depth == 3) & (side == 1), (b + 2) % 3, b)
 
-    last = 3 * pieces
-    late = (depth == 3) & (side == 0)
-    stray_shift = jnp.where(depth == 1, 1, jnp.where(late, -1, 0))
-
     def stray_received(t):
-        extra = jnp.where(late, surplus(t - last + 1), 0)
-        return clip(t + stray_shift + extra, depth * pieces)
-
-    def stray_spread(t):
-        return clip(2 * (t - pieces + 1), stray_received(t))
+        farthest = jnp.where(side == 1, t, jnp.where(t < 2 * pieces + 2, t - 4, t - 1))
+        return clip(jnp.where(depth == 1, t + 1, jnp.where(depth == 2, t - 1, farthest)), depth * pieces)
 
     def take_stray(i, carry):
         q, j = stray_order(i), i % pieces
@@ -293,45 +308,31 @@
     def late_slot(chip, lane):
         return 2 + jnp.where(lane == 1 - chip % 2, 0, 1)
 
-    def spread_stray(i, carry):
-        q, j = stray_order(i), i % pieces
-        source = stray_piece(q, j)
-        through = jnp.where(rising, 0, 1)
-
-        @pl.when(q == 0)
-        def _():
-            chip = jnp.where(side == 0, xq, yq)
-            send(source, stray_piece(through, j), tx.at[8], rx_stray.at[through, j], (z, 2 * chip + core))
-
-        @pl.when(q > 0)
-        def _():
-            chip = jnp.where(q == 1, yq, xq)
-            p = late_slot(chip, core) * pieces + j
-            send(source, col_piece(p), tx.at[8], rx_col.at[p], (z, 2 * chip + lone_core))
-
-        return carry
+    through = jnp.where(rising, 0, 1)
+
+    def spread_far(j):
+        chip = jnp.where(j < early, xq, yq)
+        send(stray_piece(0, j), stray_piece(through, j), tx.at[8], rx_stray.at[through, j], (z, 2 * chip + core))
+
+    def spread_near(q, chip, j):
+        send_col(stray_piece(q, j), late_slot(chip, core), j, 8, (z, 2 * chip + lone_core))
 
     def split_into(value, lead, trail, start):
         leading = value.astype(jnp.bfloat16)
         lead[pl.ds(start, shard_rows), :] = leading
         trail[pl.ds(start, shard_rows), :] = (value - leading.astype(jnp.float32)).astype(jnp.bfloat16)
 
-    def acc_copy(k, start):
+    def acc_copy(bank, k, start):
         return pltpu.make_async_copy(
-            acc.at[k],
+            acc.at[bank, k],
             out.at[k, :, pl.ds(pl.multiple_of(start, shard_rows), shard_rows)],
-            acc_sem.at[k],
+            acc_sem.at[bank, k],
         )
 
-    quanta = row_blocks + perturbations
+    quanta = 2 * perturbations
     base = pieces + early + 3
-    times = []
-    for gap in (0, 1, 1, 2, 3, 3, 4, 5, 6, 6, 7, 8, 8, 9):
-        times.append(base + gap)
-    for gap in (11, 11, 10, 10, 9, 8, 7):
-        times.append(last - gap)
-    for gap in (6, 6, 5, 5, 4, 3, 1):
-        times.append(last - gap)
+    times = [base + gap for gap in (0, 0, 1, 2, 2, 3, 4, 5, 5, 6, 7, 7)]
+    times += [last - gap for gap in (12, 11, 11, 10, 10, 9, 8, 7, 4, 3, 1, 0)]
     compute_lag = jnp.where(diagonal, 0, jnp.where(lone, 1, distance - 1))
 
     def done(t):
@@ -357,18 +358,24 @@
         return pl.ds(pl.multiple_of(block * block_rows, block_rows), block_rows)
 
     def quantum(g, carry):
-        slot, q = g // quanta, g % quanta
-        opening = q < row_blocks
-        kind = jnp.where(opening, 0, q - row_blocks + 1)
+        h = g - 2 * quanta
+        tail_slot = jnp.where(h < quanta, h // perturbations, h % 2) + 2
+        tail_q = jnp.where(h < quanta, h % perturbations, perturbations + (h - quanta) // 2)
+        slot = jnp.where(h < 0, g // quanta, tail_slot)
+        q = jnp.where(h < 0, g % quanta, tail_q)
+        opening = q < perturbations
+        k = q % perturbations
+        kind = jnp.where(opening, 0, k + 1)
+        bank = slot % 2
         quarter, lane = order(slot)
         place = (2 * (quarter % 2) + lane) * shard_rows
 
-        @pl.when((q == 0) | (q >= row_blocks))
-        def _():
-            @pl.when(lone & (slot >= 2))
+        @pl.when((q == 0) | (q >= perturbations))
+        def _():
+            @pl.when((z != w) & ((slot == 3) | (lone & (slot == 2))))
             def _():
                 def late_wait(j, carry):
-                    wait_col(slot * pieces + kind * CUTS + j)
+                    wait_col(slot, kind * CUTS + j)
                     return carry
 
                 lax.fori_loop(0, CUTS, late_wait, 0)
@@ -388,29 +395,27 @@
 
             split_into(stage[0], col_lead, col_trail, 0)
 
-        @pl.when((q == 0) & (slot >= 1))
-        def _():
-            for k in range(perturbations):
-                acc_copy(k, place).wait()
+        @pl.when((q == 0) & (slot >= 2))
+        def _():
+            for late in range(perturbations):
+                acc_copy(bank, late, place).wait()
 
         @pl.when(opening)
         def _():
-            def start(k, carry):
-                acc[k, target(q), :] = total(k + 1, q)
+            def start(block, carry):
+                acc[bank, k, target(block), :] = total(k + 1, block)
                 return carry
 
-            lax.fori_loop(0, perturbations, start, 0)
-
-        @pl.when(q >= row_blocks)
-        def _():
-            k = q - row_blocks
-
+            lax.fori_loop(0, row_blocks, start, 0)
+
+        @pl.when(q >= perturbations)
+        def _():
             def finish(block, carry):
-                acc[k, target(block), :] += total(0, block)
+                acc[bank, k, target(block), :] += total(0, block)
                 return carry
 
             lax.fori_loop(0, row_blocks, finish, 0)
-            acc_copy(k, place).start()
+            acc_copy(bank, k, place).start()
 
         return carry
 
@@ -449,8 +454,7 @@
 
         @pl.when(diagonal)
         def _():
-            opened = jnp.where(match, pieces, 0)
-            lax.fori_loop(jnp.where(t == 0, opened, sent(t - 1)), sent(t), emit_own, 0)
+            lax.fori_loop(sent(t - 1), sent(t), emit_own, 0)
 
         @pl.when(z != w)
         def _():
@@ -459,30 +463,45 @@
         @pl.when(inbound)
         def _():
             lax.fori_loop(stray_received(t - 1), stray_received(t), take_stray, 0)
-            lax.fori_loop(stray_spread(t - 1), stray_spread(t), spread_stray, 0)
+            far = t - pieces - 2
+            near = t - pieces - early - 2
+            near_x = near - jnp.where(side == 0, early, 0)
+            near_y = near - jnp.where(side == 1, early, 0)
+
+            @pl.when((far >= 0) & (far < pieces))
+            def _():
+                spread_far(far)
+
+            @pl.when((depth > 1) & (near_y >= 0) & (near_y < pieces))
+            def _():
+                spread_near(1, yq, near_y)
+
+            @pl.when((depth > 2) & (near_x >= 0) & (near_x < pieces))
+            def _():
+                spread_near(2, xq, near_x)
 
         @pl.when(outer & (depth == 1) & (t >= pieces) & (t < 2 * pieces))
         def _():
             j = t - pieces
             send(row_piece(xq, core, j), stray_piece(1, j), tx.at[7], rx_stray.at[1, j], onward_dev)
 
-        @pl.when(outer & (depth == 2) & (side == 0) & (t >= 2 * pieces) & (t < 2 * pieces + early))
+        @pl.when(outer & (depth == 2) & (side == 0) & (t >= 2 * pieces - 2) & (t < 2 * pieces + early - 2))
         def _():
             for shift in range(2):
-                j = 2 * (t - 2 * pieces) + shift
+                j = 2 * (t - 2 * pieces + 2) + shift
                 send(row_piece(w, core, j), stray_piece(2, j), tx.at[7], rx_stray.at[2, j], onward_dev)
 
-        hop = t - pieces - early - 2
-
-        @pl.when(relay & (hop >= 0) & (hop < pieces))
-        def _():
-            for through, chip, lone_at, here, slot in ((0, 0, 1, has_down, 9), (1, 3, 0, has_up, 10)):
+        hop = t - pieces - early - 4
+
+        @pl.when(relay & (hop >= 0) & (hop < early))
+        def _():
+            for way, chip, lone_at, x_side, here in ((0, 0, 1, 2, has_down), (1, 3, 0, 1, has_up)):
                 @pl.when(here)
                 def _():
-                    ref = stray_piece(through, hop)
-                    arrived(ref, rx_stray.at[through, hop])
-                    p = late_slot(chip, core) * pieces + hop
-                    send(ref, col_piece(p), tx.at[slot], rx_col.at[p], (z, 2 * chip + lone_at))
+                    j = hop + jnp.where(w == x_side, 0, early)
+                    ref = stray_piece(way, j)
+                    arrived(ref, rx_stray.at[way, j])
+                    send_col(ref, late_slot(chip, core), j, 10 + way, (z, 2 * chip + lone_at))
 
         m = jnp.where(t < pieces + early + 1, t - pieces - 1, t - pieces - early + 5)
 
@@ -504,10 +523,11 @@
         lax.fori_loop(done(t - 1), done(t), quantum, 0)
         return carry
 
-    lax.fori_loop(0, last + 2, step, 0)
-
-    for k in range(perturbations):
-        acc_copy(k, 0).wait()
+    lax.fori_loop(0, last + 3, step, 0)
+
+    for bank in range(2):
+        for k in range(perturbations):
+            acc_copy(bank, k, 0).wait()
 
     def drain(slot, ref):
         pltpu.make_async_copy(ref, ref, tx.at[slot]).wait()
@@ -522,15 +542,16 @@
     drain(2, rowbuf.at[0, pl.ds(0, kinds // 2)])
     drain(3, rowbuf.at[0, pl.ds(0, kinds // 2)])
     drain(4, rowbuf.at[pl.ds(0, 4)])
-    drain_shards(5, 4, has_up & (z >= w) & (core == 0))
-    drain_shards(5, 2, has_up & (z >= w) & (core == 1))
-    drain_shards(6, 4, has_down & (z <= w) & (core == 1))
-    drain_shards(6, 2, has_down & (z <= w) & (core == 0))
+    drain_shards(5, 3, has_up & (z >= w))
+    drain_shards(6, 3, has_down & (z <= w))
     for count in (1, 2, 3):
         drain_shards(7, count, outer & (depth == count - 1))
         drain_shards(8, count, outer & (depth == count))
-    drain_shards(9, 1, relay & has_down)
-    drain_shards(10, 1, relay & has_up)
+    drain_shards(9, 1, lone)
+    for way, here in ((0, has_down), (1, has_up)):
+        @pl.when(relay & here)
+        def _():
+            drain(10 + way, rowbuf.at[0, pl.ds(0, kinds // 2)])
 
 
 def panels(response_coeffs, occupied_coeffs):
@@ -544,7 +565,7 @@
         out_shape=(
             jax.ShapeDtypeStruct((perturbations, 8 * shard_rows, 4 * shard_rows), float32),
             jax.ShapeDtypeStruct((8, kinds, shard_rows, orbitals), float32),
-            jax.ShapeDtypeStruct((4, kinds, shard_rows, orbitals), float32),
+            jax.ShapeDtypeStruct((5, kinds, shard_rows, orbitals), float32),
             jax.ShapeDtypeStruct((3, kinds, shard_rows, orbitals), float32),
         ),
         in_specs=[any_space] * 2,
@@ -555,13 +576,13 @@
             pltpu.VMEM((shard_rows, orbitals), bfloat16),
             pltpu.VMEM((shard_rows, orbitals), bfloat16),
             pltpu.VMEM((kinds, shard_rows, orbitals), float32),
-            pltpu.VMEM((perturbations, 8 * shard_rows, shard_rows), float32),
+            pltpu.VMEM((2, perturbations, 8 * shard_rows, shard_rows), float32),
             pltpu.SemaphoreType.DMA((8, pieces)),
-            pltpu.SemaphoreType.DMA((4 * pieces,)),
+            pltpu.SemaphoreType.DMA((5, pieces)),
             pltpu.SemaphoreType.DMA((3, pieces)),
-            pltpu.SemaphoreType.DMA((11,)),
+            pltpu.SemaphoreType.DMA((12,)),
             pltpu.SemaphoreType.DMA((2,)),
-            pltpu.SemaphoreType.DMA((perturbations,)),
+            pltpu.SemaphoreType.DMA((2, perturbations)),
         ],
         compiler_params=pltpu.CompilerParams(
             collective_id=0, has_side_effects=True, vmem_limit_bytes=66_000_000

time: 433 us -> 351 us (0.81)
  Pallas kernels: 414 us -> 332 us
    pallas_call x1, Pallas kernels: 414 us -> 332 us  [panels(): pl.pallas_call(panel_kernel, out_shape=(jax.ShapeDtypeStruct((perturbatio...]
where the time goes in v2:
time: 351 us; the launch traced here: 350 us
  Pallas kernels  332 us (95%)
  local copies, waits for them, and re-layouts  17.7 us (5%)
    pallas_call x1, Pallas kernels, panels(): pl.pallas_call(panel_kernel, out_shape=(jax.ShapeDtypeStruct((perturbatio...  332 us
    unnamed x1, local copies, waits for them, and re-layouts  17.7 us

profile of v2, /device:TPU:29, one launch (start us, length us, event | category | flops | bytes accessed | tf_op | source)
XLA Modules:
  0.0 349.7 jit_solution(7006871012676081392)
XLA Ops:
  0.0 332.0 %shard_map.28 = (f32[3,2048,1024]{2,1,0:T(8,128)}, f32[8,4,256,1024]{3,2,1,0:T(8,128)}, f32[5,4,256,1024]{3,2,1,0:T(8,128)}, f32[3,4,256,1024]{3,2,1,0:T(8,128)}) custom-call(f32[3,256,1024]{2,1,0:T(8,128)} %resp.1, f32[256,1024]{1,0:T(8,128)} %occ.1), custom_call_target="tpu_custom_call" | custom-call | tf_op jit(solution)/shard_map/pallas_call | solution.py:563
  332.0 17.7 %copy.4 = f32[3,2048,1024]{2,1,0:T(8,128)} copy(f32[3,2048,1024]{2,1,0:T(8,128)} %get-tuple-element.6) | data formatting | bytes 50331648

commit v3 on v2

--- a/solution.py
+++ b/solution.py
@@ -93,8 +93,8 @@
 
 def panel_kernel(
     resp, occ, out, rowbuf, colbuf, straybuf,
-    row_lead, row_trail, col_lead, col_trail, stage, acc,
-    rx_row, rx_col, rx_stray, tx, stage_sem, acc_sem,
+    row_lead, row_trail, col_lead, col_trail, stage,
+    rx_row, rx_col, rx_stray, tx, stage_sem,
 ):
     perturbations, shard_rows, orbitals = resp.shape
     kinds = perturbations + 1
@@ -130,6 +130,10 @@
     onward = outer & (depth < planes - 1)
     relay = (w == 1) | (w == 2)
 
+    ending = ((z == planes - 1) | (z == 0)) & jnp.logical_not(diagonal)
+    scale = CUTS // 4
+    hop = scale
+
     barrier = pltpu.get_barrier_semaphore()
 
     def greet(device):
@@ -182,10 +186,14 @@
     def send_col(source, slot, j, way, device):
         send(source, col_piece(slot, j), tx.at[way], rx_col.at[slot, j], device)
 
-    load_resp = pltpu.make_async_copy(resp, stage.at[pl.ds(1, perturbations)], stage_sem.at[0])
-    load_occ = pltpu.make_async_copy(occ, stage.at[0], stage_sem.at[1])
-    load_resp.start()
-    load_occ.start()
+    def held(k):
+        return out.at[0, pl.ds(k * shard_rows, shard_rows)]
+
+    own = [occ] + [resp.at[k] for k in range(perturbations)]
+    loads = [pltpu.make_async_copy(own[k], held(k), stage_sem.at[k]) for k in range(kinds)]
+    keeps = [pltpu.make_async_copy(held(k), rowbuf.at[2 * w + core, k], stage_sem.at[k]) for k in range(kinds)]
+    for load in loads:
+        load.start()
 
     def launch(source, j):
         for slot, device in ((0, x_dev), (1, y_dev), (4, p_dev)):
@@ -213,11 +221,11 @@
 
     lax.fori_loop(0, CUTS, launch_occ, 0)
     lax.fori_loop(CUTS, pieces, launch_resp, 0)
-    load_resp.wait()
-    load_occ.wait()
-    keep = pltpu.make_async_copy(stage, rowbuf.at[2 * w + core], stage_sem.at[0])
-    keep.start()
-    keep.wait()
+    for load, keep in zip(loads, keeps):
+        load.wait()
+        keep.start()
+    for keep in keeps:
+        keep.wait()
 
     first = jnp.where(match, w, yq)
     second = flip(first)
@@ -284,15 +292,17 @@
         return clip(jnp.where(match, pieces + t + 1, slow), last)
 
     def received(t):
-        return clip(t - distance + 2, last)
+        return clip(t - hop * (distance - 1) + 1, last)
 
     def stray_order(i):
         b = i // pieces
         return jnp.where((depth == 3) & (side == 1), (b + 2) % 3, b)
 
     def stray_received(t):
-        farthest = jnp.where(side == 1, t, jnp.where(t < 2 * pieces + 2, t - 4, t - 1))
-        return clip(jnp.where(depth == 1, t + 1, jnp.where(depth == 2, t - 1, farthest)), depth * pieces)
+        near_end = 2 * (pieces + scale)
+        late = jnp.where(t < near_end, t - (3 * hop + 2) + (1 if scale == 1 else 0), t - 2 * scale + 1)
+        farthest = jnp.where(side == 1, t, late)
+        return clip(jnp.where(depth == 1, t + 1, jnp.where(depth == 2, t - hop, farthest)), depth * pieces)
 
     def take_stray(i, carry):
         q, j = stray_order(i), i % pieces
@@ -322,24 +332,29 @@
         lead[pl.ds(start, shard_rows), :] = leading
         trail[pl.ds(start, shard_rows), :] = (value - leading.astype(jnp.float32)).astype(jnp.bfloat16)
 
-    def acc_copy(bank, k, start):
-        return pltpu.make_async_copy(
-            acc.at[bank, k],
-            out.at[k, :, pl.ds(pl.multiple_of(start, shard_rows), shard_rows)],
-            acc_sem.at[bank, k],
-        )
-
-    quanta = 2 * perturbations
-    base = pieces + early + 3
-    times = [base + gap for gap in (0, 0, 1, 2, 2, 3, 4, 5, 5, 6, 7, 7)]
-    times += [last - gap for gap in (12, 11, 11, 10, 10, 9, 8, 7, 4, 3, 1, 0)]
-    compute_lag = jnp.where(diagonal, 0, jnp.where(lone, 1, distance - 1))
+    opening_units = 1 + perturbations * row_blocks
+    closing_units = 1 + row_blocks
+    half_units = 1 + 3 * perturbations
+    halves = 4
+    own_block = w // 2
+
+    due = []
+    for start in (19.6, 26.7, 29.9, 33.1):
+        due += [start + 0.32 * unit for unit in range(half_units)]
+    due += [36.4 + 0.3 * unit for unit in range(2 * opening_units)]
+    shown = [40.6, 41.6, 44.4, 45.4, 48, 48]
+    hidden = [44.4, 45.4, 49, 49, 49, 49]
+    due_early = due + [start + 0.3 * unit for start in shown for unit in range(closing_units)]
+    due_late = due + [start + 0.3 * unit for start in hidden for unit in range(closing_units)]
+    lag = jnp.where(diagonal, 0, jnp.maximum(hop * (distance - 1), jnp.where(lone, scale, 0)))
 
     def done(t):
         count = 0
-        for time in times:
-            count = count + jnp.where(t - compute_lag >= time, 1, 0)
-        return count
+        for soon, later in zip(due_early, due_late):
+            soon, later = min(int(soon * scale), last), int(later * scale)
+            time = soon if soon == later else jnp.where(ending, soon, later)
+            count = count + jnp.where(t - lag >= time, 1, 0)
+        return jnp.where(t >= last + 3 * scale - 1, len(due_early), count)
 
     def block_of(ref, kind, block):
         return ref[pl.ds(pl.multiple_of(kind * panel_rows + block * block_rows, block_rows), block_rows), :]
@@ -358,19 +373,25 @@
         return pl.ds(pl.multiple_of(block * block_rows, block_rows), block_rows)
 
     def quantum(g, carry):
-        h = g - 2 * quanta
-        tail_slot = jnp.where(h < quanta, h // perturbations, h % 2) + 2
-        tail_q = jnp.where(h < quanta, h % perturbations, perturbations + (h - quanta) // 2)
-        slot = jnp.where(h < 0, g // quanta, tail_slot)
-        q = jnp.where(h < 0, g % quanta, tail_q)
-        opening = q < perturbations
-        k = q % perturbations
+        half, x = g // half_units, g % half_units
+        y = x - 1 - perturbations
+        h = g - halves * half_units
+        early_work = h < 0
+        e = h - 2 * opening_units
+        slot = jnp.where(early_work, half // 2, jnp.where(e < 0, h // opening_units, (e // closing_units) % 2) + 2)
+        closing = e % closing_units
+        begin = h % opening_units
+        opening = jnp.where(early_work, y < 0, e < 0)
+        fetching = jnp.where(early_work, (x == 0) | ((y >= 0) & (y % 2 == 0)), jnp.where(e < 0, begin == 0, closing == 0))
+        early_k = jnp.where(y < 0, x - 1, y // 2)
+        k = jnp.where(early_work, early_k, jnp.where(e < 0, (begin - 1) // row_blocks, e // (2 * closing_units)))
+        early_block = jnp.where(half % 2 == 0, own_block, 1 - own_block)
+        block = jnp.where(early_work, early_block, jnp.where(e < 0, (begin - 1) % row_blocks, closing - 1))
         kind = jnp.where(opening, 0, k + 1)
-        bank = slot % 2
         quarter, lane = order(slot)
-        place = (2 * (quarter % 2) + lane) * shard_rows
-
-        @pl.when((q == 0) | (q >= perturbations))
+        place = pl.ds(pl.multiple_of((2 * (quarter % 2) + lane) * shard_rows, shard_rows), shard_rows)
+
+        @pl.when(fetching)
         def _():
             @pl.when((z != w) & ((slot == 3) | (lone & (slot == 2))))
             def _():
@@ -380,42 +401,35 @@
 
                 lax.fori_loop(0, CUTS, late_wait, 0)
 
-            def fetch(source):
-                copy = pltpu.make_async_copy(source, stage.at[0], stage_sem.at[0])
-                copy.start()
-                copy.wait()
-
-            @pl.when(diagonal)
-            def _():
-                fetch(rowbuf.at[2 * quarter + lane, kind])
-
-            @pl.when(z != w)
-            def _():
-                fetch(colbuf.at[slot, kind])
-
-            split_into(stage[0], col_lead, col_trail, 0)
-
-        @pl.when((q == 0) & (slot >= 2))
-        def _():
-            for late in range(perturbations):
-                acc_copy(bank, late, place).wait()
-
-        @pl.when(opening)
-        def _():
-            def start(block, carry):
-                acc[bank, k, target(block), :] = total(k + 1, block)
-                return carry
-
-            lax.fori_loop(0, row_blocks, start, 0)
-
-        @pl.when(q >= perturbations)
-        def _():
-            def finish(block, carry):
-                acc[bank, k, target(block), :] += total(0, block)
-                return carry
-
-            lax.fori_loop(0, row_blocks, finish, 0)
-            acc_copy(bank, k, place).start()
+            def fetch(kind, way):
+                @pl.when(diagonal)
+                def _():
+                    pltpu.make_async_copy(rowbuf.at[2 * quarter + lane, kind], stage.at[way], stage_sem.at[way]).start()
+
+                @pl.when(z != w)
+                def _():
+                    pltpu.make_async_copy(colbuf.at[slot, kind], stage.at[way], stage_sem.at[way]).start()
+
+            way = jnp.where(early_work, kind % 2, 0)
+
+            @pl.when((kind == 0) | jnp.logical_not(early_work))
+            def _():
+                fetch(kind, way)
+
+            @pl.when(early_work & (kind < perturbations))
+            def _():
+                fetch(kind + 1, 1 - way)
+
+            arrived(stage.at[way], stage_sem.at[way])
+            split_into(stage[way], col_lead, col_trail, 0)
+
+        @pl.when(opening & jnp.logical_not(fetching))
+        def _():
+            out[k, target(block), place] = total(k + 1, block)
+
+        @pl.when(jnp.logical_not(opening | fetching))
+        def _():
+            out[k, target(block), place] += total(0, block)
 
         return carry
 
@@ -465,12 +479,16 @@
             lax.fori_loop(stray_received(t - 1), stray_received(t), take_stray, 0)
             far = t - pieces - 2
             near = t - pieces - early - 2
-            near_x = near - jnp.where(side == 0, early, 0)
-            near_y = near - jnp.where(side == 1, early, 0)
-
-            @pl.when((far >= 0) & (far < pieces))
+            near_x = jnp.where(side == 0, t - 2 * (pieces + scale), near)
+            near_y = jnp.where(side == 1, t - 2 * pieces - 2, near)
+
+            @pl.when((far >= 0) & (far < jnp.where(side == 0, early, pieces)))
             def _():
                 spread_far(far)
+
+            @pl.when((side == 0) & (far >= 0) & (far < early))
+            def _():
+                spread_far(far + early)
 
             @pl.when((depth > 1) & (near_y >= 0) & (near_y < pieces))
             def _():
@@ -485,49 +503,57 @@
             j = t - pieces
             send(row_piece(xq, core, j), stray_piece(1, j), tx.at[7], rx_stray.at[1, j], onward_dev)
 
-        @pl.when(outer & (depth == 2) & (side == 0) & (t >= 2 * pieces - 2) & (t < 2 * pieces + early - 2))
+        @pl.when(outer & (depth == 2) & (side == 0) & (t >= 2 * (pieces - scale)) & (t < 2 * (pieces - scale) + early))
         def _():
             for shift in range(2):
-                j = 2 * (t - 2 * pieces + 2) + shift
+                j = 2 * (t - 2 * (pieces - scale)) + shift
                 send(row_piece(w, core, j), stray_piece(2, j), tx.at[7], rx_stray.at[2, j], onward_dev)
 
-        hop = t - pieces - early - 4
-
-        @pl.when(relay & (hop >= 0) & (hop < early))
+        turn = t - pieces - early - 2 * scale - 2
+
+        @pl.when(relay & (turn >= 0) & (turn < early))
         def _():
             for way, chip, lone_at, x_side, here in ((0, 0, 1, 2, has_down), (1, 3, 0, 1, has_up)):
                 @pl.when(here)
                 def _():
-                    j = hop + jnp.where(w == x_side, 0, early)
+                    j = turn + jnp.where(w == x_side, 0, early)
                     ref = stray_piece(way, j)
                     arrived(ref, rx_stray.at[way, j])
                     send_col(ref, late_slot(chip, core), j, 10 + way, (z, 2 * chip + lone_at))
 
-        m = jnp.where(t < pieces + early + 1, t - pieces - 1, t - pieces - early + 5)
-
-        @pl.when((m >= 0) & (m < 8) & ((m >= 6) == (t >= pieces + early + 1)))
-        def _():
+        def load(task):
+            m, kind = task // kinds, task % kinds
             quarter = jnp.where(m < 2, w, jnp.where(m < 4, xq, jnp.where(m < 6, yq, dq)))
-            shard = 2 * quarter + m % 2
-            copy = pltpu.make_async_copy(rowbuf.at[shard], stage, stage_sem.at[0])
-            copy.start()
+            shard, way = 2 * quarter + m % 2, task % 2
+            copy = pltpu.make_async_copy(rowbuf.at[shard, kind], stage.at[way], stage_sem.at[way])
+            return copy, way, kind * panel_rows + shard * shard_rows
+
+        def convert(task, carry):
+            copy, way, start = load(task)
+
+            @pl.when((task == 0) | (task == 6 * kinds))
+            def _():
+                copy.start()
+
+            @pl.when((task + 1 != 6 * kinds) & (task + 1 < 8 * kinds))
+            def _():
+                load(task + 1)[0].start()
+
             copy.wait()
-
-            def convert(k, carry):
-                start = pl.multiple_of(k * panel_rows + shard * shard_rows, shard_rows)
-                split_into(stage[k], row_lead, row_trail, start)
-                return carry
-
-            lax.fori_loop(0, kinds, convert, 0)
-
-        lax.fori_loop(done(t - 1), done(t), quantum, 0)
+            split_into(stage[way], row_lead, row_trail, pl.multiple_of(start, shard_rows))
+            return carry
+
+        def converted(t):
+            near_tasks = clip((t - pieces) * 8 // scale, 6 * kinds)
+            return near_tasks + clip((t - pieces - early) * 4 // scale, 2 * kinds)
+
+        lax.fori_loop(converted(t - 1), converted(t), convert, 0)
+        ready = done(t)
+        lax.fori_loop(carry, ready, quantum, 0)
+        carry = ready
         return carry
 
-    lax.fori_loop(0, last + 3, step, 0)
-
-    for bank in range(2):
-        for k in range(perturbations):
-            acc_copy(bank, k, 0).wait()
+    lax.fori_loop(0, last + 3 * scale, step, 0)
 
     def drain(slot, ref):
         pltpu.make_async_copy(ref, ref, tx.at[slot]).wait()
@@ -563,37 +589,54 @@
     return pl.pallas_call(
         panel_kernel,
         out_shape=(
-            jax.ShapeDtypeStruct((perturbations, 8 * shard_rows, 4 * shard_rows), float32),
+            pltpu.VMEM((perturbations, 8 * shard_rows, 4 * shard_rows), float32),
             jax.ShapeDtypeStruct((8, kinds, shard_rows, orbitals), float32),
             jax.ShapeDtypeStruct((5, kinds, shard_rows, orbitals), float32),
             jax.ShapeDtypeStruct((3, kinds, shard_rows, orbitals), float32),
         ),
         in_specs=[any_space] * 2,
-        out_specs=(any_space,) * 4,
+        out_specs=(pl.BlockSpec(memory_space=pltpu.VMEM),) + (any_space,) * 3,
         scratch_shapes=[
             pltpu.VMEM((kinds * 8 * shard_rows, orbitals), bfloat16),
             pltpu.VMEM((kinds * 8 * shard_rows, orbitals), bfloat16),
             pltpu.VMEM((shard_rows, orbitals), bfloat16),
             pltpu.VMEM((shard_rows, orbitals), bfloat16),
-            pltpu.VMEM((kinds, shard_rows, orbitals), float32),
-            pltpu.VMEM((2, perturbations, 8 * shard_rows, shard_rows), float32),
+            pltpu.VMEM((2, shard_rows, orbitals), float32),
             pltpu.SemaphoreType.DMA((8, pieces)),
             pltpu.SemaphoreType.DMA((5, pieces)),
             pltpu.SemaphoreType.DMA((3, pieces)),
             pltpu.SemaphoreType.DMA((12,)),
-            pltpu.SemaphoreType.DMA((2,)),
-            pltpu.SemaphoreType.DMA((2, perturbations)),
+            pltpu.SemaphoreType.DMA((kinds,)),
         ],
         compiler_params=pltpu.CompilerParams(
-            collective_id=0, has_side_effects=True, vmem_limit_bytes=66_000_000
+            collective_id=0, has_side_effects=True, vmem_limit_bytes=41_300_000
         ),
     )(response_coeffs, occupied_coeffs)[0]
+
+
+def store_kernel(held, out, sem):
+    copies = [pltpu.make_async_copy(held.at[k], out.at[k], sem.at[k]) for k in range(held.shape[0])]
+    for copy in copies:
+        copy.start()
+    for copy in copies:
+        copy.wait()
+
+
+def store(held):
+    return pl.pallas_call(
+        store_kernel,
+        out_shape=jax.ShapeDtypeStruct(held.shape, held.dtype),
+        in_specs=[pl.BlockSpec(memory_space=pltpu.VMEM)],
+        out_specs=pl.BlockSpec(memory_space=pl.ANY),
+        scratch_shapes=[pltpu.SemaphoreType.DMA((held.shape[0],))],
+        compiler_params=pltpu.CompilerParams(vmem_limit_bytes=1_000_000),
+    )(held)
 
 
 def solution(mesh):
     fits = mesh.shape["row"] == 4 and mesh.shape["col"] == 8
     return jax.shard_map(
-        panels if fits else shards,
+        (lambda *args: store(panels(*args))) if fits else shards,
         mesh=mesh,
         in_specs=(P(None, ("row", "col"), None), P(("row", "col"), None)),
         out_specs=P(None, "row", "col"),

time: 351 us -> 332 us (0.946); the launches traced: 350 us -> 327 us
  local copies, waits for them, and re-layouts: 17.7 us -> 0 us
  Pallas kernels: 332 us -> 327 us
    unnamed x1 -> x0, local copies, waits for them, and re-layouts: 17.7 us -> none
    pallas_call x1 -> x2, Pallas kernels: 332 us -> 327 us  [the longest x1 318 us: panels(): pl.pallas_call(panel_kernel, out_shape=(pltpu.VMEM((perturbations, 8 * sh...]
where the time goes in v3:
time: 332 us; the launch traced here: 327 us
  Pallas kernels  327 us (98%)
    pallas_call x1, Pallas kernels, panels(): pl.pallas_call(panel_kernel, out_shape=(pltpu.VMEM((perturbations, 8 * sh...  318 us
    pallas_call x1, Pallas kernels, store(): pl.pallas_call(store_kernel, out_shape=jax.ShapeDtypeStruct(held.shape, h...  8.71 us

profile of v3, /device:TPU:29, one launch (start us, length us, event | category | flops | bytes accessed | tf_op | source)
XLA Modules:
  0.0 327.1 jit_solution(8406675691023250329)
XLA Ops:
  0.0 318.4 %shard_map.28 = (f32[3,2048,1024]{2,1,0:T(8,128)S(1)}, f32[8,4,256,1024]{3,2,1,0:T(8,128)}, f32[5,4,256,1024]{3,2,1,0:T(8,128)}, f32[3,4,256,1024]{3,2,1,0:T(8,128)}) custom-call(f32[3,256,1024]{2,1,0:T(8,128)} %resp.1, f32[256,1024]{1,0:T(8,128)} %occ.1), custom_call_target="tpu_custom_call" | custom-call | tf_op jit(solution)/shard_map/pallas_call | solution.py:589
  318.4 8.7 %shard_map.29 = f32[3,2048,1024]{2,1,0:T(8,128)} custom-call(f32[3,2048,1024]{2,1,0:T(8,128)S(1)} %get-tuple-element.6.held), custom_call_target="tpu_custom_call" | custom-call | tf_op jit(solution)/shard_map/pallas_call | solution.py:626

commit v4 on v3

--- a/solution.py
+++ b/solution.py
@@ -81,6 +81,7 @@
 
 
 CUTS = 4
+STORES = 4
 
 
 def flip(value):
@@ -343,7 +344,7 @@
         due += [start + 0.32 * unit for unit in range(half_units)]
     due += [36.4 + 0.3 * unit for unit in range(2 * opening_units)]
     shown = [40.6, 41.6, 44.4, 45.4, 48, 48]
-    hidden = [44.4, 45.4, 49, 49, 49, 49]
+    hidden = [42.5, 44, 46, 47.5, 49, 49]
     due_early = due + [start + 0.3 * unit for start in shown for unit in range(closing_units)]
     due_late = due + [start + 0.3 * unit for start in hidden for unit in range(closing_units)]
     lag = jnp.where(diagonal, 0, jnp.maximum(hop * (distance - 1), jnp.where(lone, scale, 0)))
@@ -401,7 +402,9 @@
 
                 lax.fori_loop(0, CUTS, late_wait, 0)
 
-            def fetch(kind, way):
+            def fetch(slot, kind, way):
+                quarter, lane = order(slot)
+
                 @pl.when(diagonal)
                 def _():
                     pltpu.make_async_copy(rowbuf.at[2 * quarter + lane, kind], stage.at[way], stage_sem.at[way]).start()
@@ -410,15 +413,19 @@
                 def _():
                     pltpu.make_async_copy(colbuf.at[slot, kind], stage.at[way], stage_sem.at[way]).start()
 
-            way = jnp.where(early_work, kind % 2, 0)
-
-            @pl.when((kind == 0) | jnp.logical_not(early_work))
-            def _():
-                fetch(kind, way)
-
-            @pl.when(early_work & (kind < perturbations))
-            def _():
-                fetch(kind + 1, 1 - way)
+            way = jnp.where(early_work, kind % 2, slot % 2)
+            begins = jnp.logical_not(diagonal) | ((slot == 2) & (kind == 0))
+            goes_on = diagonal & ((slot == 2) | (kind < perturbations))
+            next_slot = jnp.where(early_work, slot, 5 - slot)
+            next_kind = jnp.where(early_work | (slot == 3), kind + 1, kind)
+
+            @pl.when(jnp.where(early_work, kind == 0, begins))
+            def _():
+                fetch(slot, kind, way)
+
+            @pl.when(jnp.where(early_work, kind < perturbations, goes_on))
+            def _():
+                fetch(next_slot, next_kind, 1 - way)
 
             arrived(stage.at[way], stage_sem.at[way])
             split_into(stage[way], col_lead, col_trail, 0)
@@ -615,7 +622,12 @@
 
 
 def store_kernel(held, out, sem):
-    copies = [pltpu.make_async_copy(held.at[k], out.at[k], sem.at[k]) for k in range(held.shape[0])]
+    rows = held.shape[1] // STORES
+    copies = []
+    for k in range(held.shape[0]):
+        for part in range(STORES):
+            at = pl.ds(part * rows, rows)
+            copies.append(pltpu.make_async_copy(held.at[k, at], out.at[k, at], sem.at[k, part]))
     for copy in copies:
         copy.start()
     for copy in copies:
@@ -628,7 +640,7 @@
         out_shape=jax.ShapeDtypeStruct(held.shape, held.dtype),
         in_specs=[pl.BlockSpec(memory_space=pltpu.VMEM)],
         out_specs=pl.BlockSpec(memory_space=pl.ANY),
-        scratch_shapes=[pltpu.SemaphoreType.DMA((held.shape[0],))],
+        scratch_shapes=[pltpu.SemaphoreType.DMA((held.shape[0], STORES))],
         compiler_params=pltpu.CompilerParams(vmem_limit_bytes=1_000_000),
     )(held)
 

time: 332 us -> 329 us (level)
  no operation moved by 1% of the time
where the time goes in v4:
time: 329 us; the launch traced here: 326 us
  Pallas kernels  326 us (99%)
    pallas_call x1, Pallas kernels, panels(): pl.pallas_call(panel_kernel, out_shape=(pltpu.VMEM((perturbations, 8 * sh...  317 us
    pallas_call x1, Pallas kernels, store(): pl.pallas_call(store_kernel, out_shape=jax.ShapeDtypeStruct(held.shape, h...  8.48 us

profile of v4, /device:TPU:29, one launch (start us, length us, event | category | flops | bytes accessed | tf_op | source)
XLA Modules:
  0.0 326.0 jit_solution(4520445410533331335)
XLA Ops:
  0.0 317.5 %shard_map.28 = (f32[3,2048,1024]{2,1,0:T(8,128)S(1)}, f32[8,4,256,1024]{3,2,1,0:T(8,128)}, f32[5,4,256,1024]{3,2,1,0:T(8,128)}, f32[3,4,256,1024]{3,2,1,0:T(8,128)}) custom-call(f32[3,256,1024]{2,1,0:T(8,128)} %resp.1, f32[256,1024]{1,0:T(8,128)} %occ.1), custom_call_target="tpu_custom_call" | custom-call | tf_op jit(solution)/shard_map/pallas_call | solution.py:596
  317.5 8.5 %shard_map.29 = f32[3,2048,1024]{2,1,0:T(8,128)} custom-call(f32[3,2048,1024]{2,1,0:T(8,128)S(1)} %get-tuple-element.6.held), custom_call_target="tpu_custom_call" | custom-call | tf_op jit(solution)/shard_map/pallas_call | solution.py:638
